TPU v7x, 128 devices: a whole 4x4x4 slice. The times are simulated.
128 devices in a mesh: seg: 32 (over y_lo, x, z), rep: 4 (over y_hi, core).
Axes of the slice: x: 4, y: 4 (y_hi: 2, y_lo: 2; y = y_hi * 2 + y_lo), z: 4, core: 2. Of those that a mesh axis runs over, the one named last changes fastest.
Arguments:
- decoder_rows: bfloat16 [256, 4096], P('rep', 'seg'), may hold values from -2000 to 2000
- norm_gain: float32 [4096], replicated, may hold values from 0.5 to 1.5
- query_weight: bfloat16 [4096, 4096], P('rep', 'seg'), may hold values from -1 to 1
- key_codes: bfloat16 [4, 16384, 4096], P('rep', 'seg'), may hold values from -127 to 127, as said below
- key_scale: float32 [4, 128, 64], P('rep', 'seg'), may hold values from 0.5 to 1.5
- value_codes: bfloat16 [4, 16384, 4096], P('rep', 'seg'), may hold values from -6 to 6
- value_scale: float32 [4, 128, 64], P('rep', 'seg'), may hold values from 0.5 to 2
- enc_lengths: int32 [4], P('rep'), may hold values from 4096 to 16384
- output_weight: bfloat16 [4096, 4096], P('seg', 'rep'), may hold values from -0.09375 to 0.09375
Outputs:
- update: bfloat16 [256, 4096], P('rep', 'seg')
Inputs may be any that keep to these rules, and one draw needn't show every extreme that they name: `key_codes`: codes of a block times its scale give the cached keys.
All inputs are finite; a program needn't handle non-finite values.
Results may differ from a plain program's by a relative error of at most 0.011.
Values may be sent and summed in bfloat16 or wider, within the bound.
No kernel may reach another device: no remote copies, remote signals or barrier semaphores. Data moves between devices by JAX's collectives and lax.ppermute only.
A program may use at most 64 MiB of HBM per device.

v0:
```python
import jax
import jax.numpy as jnp
from jax import lax
from jax.sharding import PartitionSpec as P


def laid_out(tiles, dim):
    tiles = jnp.moveaxis(tiles, 0, dim)
    dims = tiles.shape
    return tiles.reshape(*dims[:dim], dims[dim] * dims[dim + 1], *dims[dim + 2 :])


def from_everyone(shard, axis):
    count = lax.axis_size(axis)
    return lax.all_to_all(
        jnp.broadcast_to(shard[None], (count, *shard.shape)), axis, 0, 0, tiled=True
    )


def gathered_copies(shard, axis, dim):
    return laid_out(from_everyone(shard, axis), dim)


def side_by_side(arrays, axis, split_dim, concat_dim, along):
    ends, at = ([], 0)
    for a in arrays[:-1]:
        at += a.shape[along]
        ends.append(at)
    both = jnp.concatenate(arrays, axis=along)
    return tuple(
        jnp.split(
            lax.all_to_all(both, axis, split_axis=split_dim, concat_axis=concat_dim, tiled=True),
            ends,
            axis=along,
        )
    )


def in_blocks(shard, dim, count):
    before, after = (shard.shape[:dim], shard.shape[dim + 1 :])
    return jnp.moveaxis(shard.reshape(*before, count, -1, *after), dim, 0)


def sent_and_summed(shard, axis, dim):
    tiles = in_blocks(shard, dim, lax.axis_size(axis))
    arrived = lax.all_to_all(tiles, axis, split_axis=0, concat_axis=0, tiled=True)
    return arrived.sum(axis=0)


def per_device(
    decoder_rows,
    norm_gain,
    query_weight,
    key_codes,
    key_scale,
    value_codes,
    value_scale,
    enc_lengths,
    output_weight,
):
    gathered = gathered_copies(decoder_rows, "seg", 1)
    widened = gathered.astype(jnp.float32)
    variance = jnp.mean(widened * widened, axis=-1, keepdims=True)
    normed = (widened * lax.rsqrt(variance + 1e-06) * norm_gain[None, :]).astype(jnp.bfloat16)
    query_own = jnp.dot(
        normed, gathered_copies(query_weight, "rep", 0), preferred_element_type=jnp.float32
    ).astype(jnp.bfloat16)
    queries = gathered_copies(query_own, "seg", 1)
    docs_here, seg_length, inner_width = key_codes.shape
    head_count = key_scale.shape[2]
    head_dim = inner_width // head_count
    block_length = seg_length // key_scale.shape[1]
    per_doc = queries.shape[0] // docs_here
    row_count = docs_here * per_doc
    first_pos = lax.axis_index("seg") * seg_length
    positions = first_pos + jnp.arange(seg_length, dtype=jnp.int32)

    def one_doc(group_members):
        (
            document_query,
            document_keys,
            document_values,
            document_key_scale,
            document_value_scale,
            document_length,
        ) = group_members
        split_query = document_query.reshape(per_doc, head_count, head_dim)
        split_keys = document_keys.reshape(seg_length, head_count, head_dim)
        split_values = document_values.reshape(seg_length, head_count, head_dim)
        attention_scores = jnp.einsum(
            "qhd,khd->qhk", split_query, split_keys, preferred_element_type=jnp.float32
        )
        key_multiplier = jnp.repeat(document_key_scale, block_length, axis=0).T
        value_factor = jnp.repeat(document_value_scale, block_length, axis=0).T
        attention_scores = attention_scores * key_multiplier[None]
        usable = (positions < document_length)[None, None, :]
        attention_scores = jnp.where(usable, attention_scores, jnp.float32(-1e30))
        peaks = jnp.max(attention_scores, axis=-1)
        weights = jnp.where(usable, jnp.exp(attention_scores - peaks[..., None]), jnp.float32(0.0))
        totals = jnp.sum(weights, axis=-1)
        scaled = (weights * value_factor[None]).astype(jnp.bfloat16)
        attended = jnp.einsum(
            "qhk,khd->qhd", scaled, split_values, preferred_element_type=jnp.float32
        )
        return (peaks, totals, attended.reshape(per_doc, inner_width))

    query_docs = queries.reshape(docs_here, per_doc, inner_width)
    peaks, totals, outputs = lax.map(
        one_doc, (query_docs, key_codes, value_codes, key_scale, value_scale, enc_lengths)
    )
    peaks = peaks.reshape(row_count, head_count)
    totals = totals.reshape(row_count, head_count)
    outputs = outputs.reshape(row_count, inner_width)
    seg_count = lax.axis_size("seg")
    own_heads = head_count // seg_count
    received = (
        *side_by_side((peaks[None], totals[None]), "seg", 2, 0, 1),
        lax.all_to_all(outputs[None], "seg", split_axis=2, concat_axis=0, tiled=True),
    )
    peak_all, total_all, out_all = received
    largest = jnp.max(peak_all, axis=0)
    factor = jnp.exp(peak_all - largest[None])
    denominator = jnp.sum(factor * total_all, axis=0)
    numerator = jnp.sum(
        out_all.reshape(seg_count, row_count, own_heads, head_dim) * factor[..., None], axis=0
    )
    attn_own = (
        (numerator / denominator[..., None])
        .reshape(row_count, own_heads * head_dim)
        .astype(jnp.bfloat16)
    )
    partial_terms = jnp.dot(
        attn_own, gathered_copies(output_weight, "rep", 1), preferred_element_type=jnp.float32
    )
    return sent_and_summed(partial_terms, "seg", 1).astype(jnp.bfloat16)


def solution(mesh):
    placed = (
        P("rep", "seg"),
        P(),
        P("rep", "seg"),
        P("rep", "seg", None),
        P("rep", "seg", None),
        P("rep", "seg", None),
        P("rep", "seg", None),
        P("rep"),
        P("seg", "rep"),
    )
    return jax.shard_map(
        per_device, mesh=mesh, in_specs=placed, out_specs=P("rep", "seg"), check_vma=False
    )
```

profile of v0, /device:TPU:0, one launch (start us, length us, event | category | flops | bytes accessed | tf_op | source)
XLA Modules:
  0.0 186.5 jit_solution(13017367994925692182)
XLA Ops:
  0.9 20.6 %all_to_all.58 = bf16[32,64,128]{2,1,0:T(8,128)(2,1)S(1)} all-to-all(bf16[32,64,128]{2,1,0:T(8,128)(2,1)S(1)} %broadcast_in_dim.84), channel_id=1, replica_groups=mesh['seg'=32,'rep'=4] {'seg'}, dimensions={0} | all-to-all | bytes 1048576 | tf_op jit(solution)/shard_map/all_to_all | solution.py:15
  21.5 2.1 %broadcast_in_dim.85 = bf16[4,1024,128]{2,1,0:T(8,128)(2,1)} broadcast(bf16[1024,128]{1,0:T(8,128)(2,1)} %param.11), dimensions={1,2} | broadcast | bytes 1310720 | tf_op jit(solution)/shard_map/broadcast_in_dim | solution.py:16
  23.5 4.2 %all-to-all-start.1 = ((bf16[4,1024,128]{2,1,0:T(8,128)(2,1)}), bf16[4,1024,128]{2,1,0:T(8,128)(2,1)S(1)}, u32[]{:S(2)}, u32[]{:S(2)}) async-start(bf16[4,1024,128]{2,1,0:T(8,128)(2,1)} %broadcast_in_dim.85), calls=%async_computation.1 | async-start | bytes 2097152 | tf_op jit(solution)/shard_map/all_to_all | solution.py:15
  27.9 15.7 %all-to-all-done.1 = bf16[4,1024,128]{2,1,0:T(8,128)(2,1)S(1)} async-done(((bf16[4,1024,128]{2,1,0:T(8,128)(2,1)}), bf16[4,1024,128]{2,1,0:T(8,128)(2,1)S(1)}, u32[]{:S(2)}, u32[]{:S(2)}) %all-to-all-start.1) | async-done | bytes 1048608 | tf_op jit(solution)/shard_map/all_to_all | solution.py:15
  45.6 4.2 %all-to-all-start.2 = ((bf16[32,64,128]{2,1,0:T(8,128)(2,1)}), bf16[32,64,128]{2,1,0:T(8,128)(2,1)S(1)}, u32[]{:S(2)}, u32[]{:S(2)}) async-start(bf16[32,64,128]{2,1,0:T(8,128)(2,1)} %broadcast_in_dim.86), calls=%async_computation.2 | async-start | bytes 1048576 | tf_op jit(solution)/shard_map/all_to_all | solution.py:15
  50.7 6.5 %copy.40 = bf16[1,512,4096]{1,2,0:T(8,128)(2,1)} copy(bf16[1,512,4096]{2,1,0:T(8,128)(2,1)} %param.12) | data formatting | bytes 8388608 | tf_op args[3]
  57.2 6.5 %copy.45 = bf16[1,512,4096]{1,2,0:T(8,128)(2,1)} copy(bf16[1,512,4096]{2,1,0:T(8,128)(2,1)} %param.14) | data formatting | bytes 8388608 | tf_op args[5]
  64.8 4.2 %bitcast_reduce_fusion = (f32[64,64]{0,1:T(8,128)S(1)}, f32[64,64,512]{2,1,0:T(8,128)S(1)}) fusion(f32[64,512]{1,0:T(8,128)S(1)} %get-tuple-element.30, pred[512]{0:T(512)(128)(4,1)S(1)} %add_compare_fusion, bf16[512,64,64]{0,2,1:T(8,128)(2,1)} %bitcast.83, bf16[64,64,64]{2,1,0:T(8,128)(2,1)S(1)} %reshape.91), kind=kOutput, calls=%fused_computation.1 | convolution fusion | flops 274722816 | bytes 13255168 | tf_op jit(solution)/shard_map/while/body/eval_jaxpr/qhd,khd->qhk/dot_general | solution.py:90
  69.0 3.2 %copy-done = f32[64,64,512]{2,1,0:T(8,128)} copy-done((f32[64,64,512]{2,1,0:T(8,128)}, f32[64,64,512]{2,1,0:T(8,128)S(1)}, u32[]{:S(2)}) %copy-start) | copy-done | bytes 8388632
  72.2 2.8 %fusion.2 = f32[64,64]{0,1:T(8,128)S(1)} fusion(f32[64,64,512]{2,1,0:T(8,128)S(1)} %get-tuple-element.28, f32[64,64]{0,1:T(8,128)S(1)} %get-tuple-element.27, f32[64,512]{1,0:T(8,128)S(1)} %get-tuple-element.30, pred[512]{0:T(512)(128)(4,1)S(1)} %add_compare_fusion), kind=kLoop, calls=%fused_computation.6 | loop fusion | flops 10481664 | bytes 8552960 | tf_op jit(solution)/shard_map/while/body/eval_jaxpr/reduce_sum | solution.py:100
  75.7 8.5 %all-to-all-start.4 = ((f32[1,128,64]{1,0,2:T(1,128)}), f32[1,128,64]{1,0,2:T(1,128)S(1)}, u32[]{:S(2)}, u32[]{:S(2)}) async-start(f32[1,128,64]{1,0,2:T(1,128)} %pad_maximum_fusion), calls=%async_computation.4 | async-start | bytes 65536 | tf_op jit(solution)/shard_map/all_to_all | solution.py:32
  84.2 8.5 %fusion.12 = f32[64,64,64]{2,0,1:T(8,128)} fusion(bf16[512,64,64]{0,2,1:T(8,128)(2,1)} %bitcast.86, f32[64,64,512]{2,1,0:T(8,128)} %copy-done, f32[64,512]{1,0:T(8,128)S(1)} %get-tuple-element.29, f32[64,64]{0,1:T(8,128)S(1)} %get-tuple-element.27, f32[64,512]{1,0:T(8,128)S(1)} %get-tuple-element.30, pred[512]{0:T(512)(128)(4,1)S(1)} %add_compare_fusion), kind=kOutput, calls=%fused_computation.17 | convolution fusion | flops 281018368 | bytes 13910528 | tf_op jit(solution)/shard_map/while/body/eval_jaxpr/qhk,khd->qhd/dot_general | solution.py:102
  92.8 2.0 %copy.50 = f32[64,64,64]{0,2,1:T(8,128)S(1)} copy(f32[64,64,64]{2,0,1:T(8,128)} %fusion.12) | data formatting | bytes 2097152 | tf_op jit(solution)/shard_map/while/body/jit(dynamic_update_index_in_dim)/broadcast_in_dim | solution.py:108
  95.2 19.4 %reduce.3 = f32[4096,64]{1,0:T(8,128)} reduce(f32[4096,1,64]{2,1,0:T(1,128)S(1)} %bitcast.84, f32[]{:T(128)} %broadcast.48), dimensions={1}, to_apply=%bitcast.73.reduce_sub_computation | reduce | bytes 2097156
  114.6 3.4 %reshape.98 = f32[32,1,8192]{2,1,0:T(1,128)} reshape(f32[4096,64]{1,0:T(8,128)} %reduce.3) | data formatting | bytes 2097152
  118.1 8.1 %all-to-all-start.3 = ((f32[32,1,8192]{2,1,0:T(1,128)}), f32[32,1,8192]{2,1,0:T(1,128)S(1)}, u32[]{:S(2)}, u32[]{:S(2)}) async-start(f32[32,1,8192]{2,1,0:T(1,128)} %reshape.98), calls=%async_computation.3 | async-start | bytes 2097152 | tf_op jit(solution)/shard_map/all_to_all | solution.py:118
  126.4 15.4 %all-to-all-done.3 = f32[32,1,8192]{2,1,0:T(1,128)S(1)} async-done(((f32[32,1,8192]{2,1,0:T(1,128)}), f32[32,1,8192]{2,1,0:T(1,128)S(1)}, u32[]{:S(2)}, u32[]{:S(2)}) %all-to-all-start.3) | async-done | bytes 1048608 | tf_op jit(solution)/shard_map/all_to_all | solution.py:118
  141.8 1.2 broadcast_in_dim.94
  142.9 4.5 %all-to-all-start.5 = ((bf16[4,128,1024]{1,2,0:T(8,128)(2,1)}), bf16[4,128,1024]{1,2,0:T(8,128)(2,1)}, u32[]{:S(2)}, u32[]{:S(2)}) async-start(bf16[4,128,1024]{1,2,0:T(8,128)(2,1)} %broadcast_in_dim.94), calls=%async_computation.5 | async-start | bytes 2097152 | tf_op jit(solution)/shard_map/all_to_all | solution.py:15
  147.6 3.2 %reduce.4 = f32[32,8192]{1,0:T(8,128)S(1)} reduce(f32[32,1,8192]{2,1,0:T(1,128)S(1)} %all-to-all-done.3, f32[]{:T(128)} %broadcast.48), dimensions={1}, to_apply=%all_to_all.42.reduce_sub_computation | reduce | bytes 2097156 | tf_op jit(solution)/shard_map/all_to_all | solution.py:118
  150.8 2.6 %reshape.99 = f32[4096,1,64]{2,1,0:T(1,128)S(1)} reshape(f32[32,8192]{1,0:T(8,128)S(1)} %reduce.4) | data formatting | bytes 2097152
  153.7 9.5 %all-to-all-done.5 = bf16[4,128,1024]{1,2,0:T(8,128)(2,1)} async-done(((bf16[4,128,1024]{1,2,0:T(8,128)(2,1)}), bf16[4,128,1024]{1,2,0:T(8,128)(2,1)}, u32[]{:S(2)}, u32[]{:S(2)}) %all-to-all-start.5) | async-done | bytes 1048608 | tf_op jit(solution)/shard_map/all_to_all | solution.py:15
  163.2 1.7 convolution_bitcast_fusion
  164.9 20.9 %all_to_all.59 = f32[32,64,128]{2,1,0:T(8,128)S(1)} all-to-all(f32[32,64,128]{2,1,0:T(8,128)S(1)} %convolution_bitcast_fusion), channel_id=1, replica_groups=mesh['seg'=32,'rep'=4] {'seg'}, dimensions={0} | all-to-all | bytes 2097152 | tf_op jit(solution)/shard_map/all_to_all | solution.py:46
  (30 shorter events, 6.8 us)
Async XLA Ops:
  0.0 49.8 %copy-start.2 = (f32[1,4,64]{2,1,0:T(4,128)S(1)}, f32[1,4,64]{2,1,0:T(4,128)}, u32[]{:S(2)}) copy-start(f32[1,4,64]{2,1,0:T(4,128)} %param.13) | copy-start | bytes 3076
  0.0 50.0 %copy-start.3 = (f32[1,4,64]{2,1,0:T(4,128)S(1)}, f32[1,4,64]{2,1,0:T(4,128)}, u32[]{:S(2)}) copy-start(f32[1,4,64]{2,1,0:T(4,128)} %param.15) | copy-start | bytes 3076
  23.5 20.1 %all-to-all-start.1 = ((bf16[4,1024,128]{2,1,0:T(8,128)(2,1)}), bf16[4,1024,128]{2,1,0:T(8,128)(2,1)S(1)}, u32[]{:S(2)}, u32[]{:S(2)}) async-start(bf16[4,1024,128]{2,1,0:T(8,128)(2,1)} %broadcast_in_dim.85), calls=%async_computation.1 | async-start | bytes 2097152 | tf_op jit(solution)/shard_map/all_to_all | solution.py:15
  45.6 18.4 %all-to-all-start.2 = ((bf16[32,64,128]{2,1,0:T(8,128)(2,1)}), bf16[32,64,128]{2,1,0:T(8,128)(2,1)S(1)}, u32[]{:S(2)}, u32[]{:S(2)}) async-start(bf16[32,64,128]{2,1,0:T(8,128)(2,1)} %broadcast_in_dim.86), calls=%async_computation.2 | async-start | bytes 1048576 | tf_op jit(solution)/shard_map/all_to_all | solution.py:15
  68.9 3.2 %copy-start = (f32[64,64,512]{2,1,0:T(8,128)}, f32[64,64,512]{2,1,0:T(8,128)S(1)}, u32[]{:S(2)}) copy-start(f32[64,64,512]{2,1,0:T(8,128)S(1)} %get-tuple-element.28) | copy-start | bytes 25165828
  75.7 42.3 %all-to-all-start.4 = ((f32[1,128,64]{1,0,2:T(1,128)}), f32[1,128,64]{1,0,2:T(1,128)S(1)}, u32[]{:S(2)}, u32[]{:S(2)}) async-start(f32[1,128,64]{1,0,2:T(1,128)} %pad_maximum_fusion), calls=%async_computation.4 | async-start | bytes 65536 | tf_op jit(solution)/shard_map/all_to_all | solution.py:32
  92.8 33.5 %copy-start.1 = (bf16[128,1024]{1,0:T(8,128)(2,1)S(1)}, bf16[128,1024]{1,0:T(8,128)(2,1)}, u32[]{:S(2)}) copy-start(bf16[128,1024]{1,0:T(8,128)(2,1)} %param.17) | copy-start | bytes 786436
  118.1 23.7 %all-to-all-start.3 = ((f32[32,1,8192]{2,1,0:T(1,128)}), f32[32,1,8192]{2,1,0:T(1,128)S(1)}, u32[]{:S(2)}, u32[]{:S(2)}) async-start(f32[32,1,8192]{2,1,0:T(1,128)} %reshape.98), calls=%async_computation.3 | async-start | bytes 2097152 | tf_op jit(solution)/shard_map/all_to_all | solution.py:118
  142.9 20.2 %all-to-all-start.5 = ((bf16[4,128,1024]{1,2,0:T(8,128)(2,1)}), bf16[4,128,1024]{1,2,0:T(8,128)(2,1)}, u32[]{:S(2)}, u32[]{:S(2)}) async-start(bf16[4,128,1024]{1,2,0:T(8,128)(2,1)} %broadcast_in_dim.94), calls=%async_computation.5 | async-start | bytes 2097152 | tf_op jit(solution)/shard_map/all_to_all | solution.py:15
where the time goes:
time: 188 us; the launch traced here: 186 us
  blocking collectives  41.5 us (22%)
  waiting for transfers between devices  40.6 us (22%)
  local copies, waits for them, and re-layouts  31.1 us (17%)
  starting transfers between devices  29.5 us (16%)
  other arithmetic  27.5 us (15%)
  matrix products  15.5 us (8%)
    all_to_all x3, waiting for transfers between devices, from_everyone(): lax.all_to_all(jnp.broadcast_to(shard[None], (count, *shard.shape)), axis...  25.2 us
    unnamed x14, local copies, waits for them, and re-layouts  23 us
    all_to_all x1, blocking collectives, sent_and_summed(): lax.all_to_all(tiles, axis, split_axis=0, concat_axis=0, tiled=True)  20.9 us
    all_to_all x1, blocking collectives, from_everyone(): lax.all_to_all(jnp.broadcast_to(shard[None], (count, *shard.shape)), axis...  20.6 us
    unnamed x1, other arithmetic  19.4 us
    all_to_all x1, waiting for transfers between devices, per_device(): lax.all_to_all(outputs[None], 'seg', split_axis=2, concat_axis=0, tiled=T...  15.4 us
    all_to_all x3, starting transfers between devices, from_everyone(): lax.all_to_all(jnp.broadcast_to(shard[None], (count, *shard.shape)), axis...  12.8 us
    dot_general x1, matrix products, one_doc(): jnp.einsum('qhk,khd->qhd', scaled, split_values, preferred_element_type=j...  8.53 us
  transfers between devices with their start and end apart: 5, of which 3 were waited for; matrix products, arithmetic and copies ran while one was open for 29% of the time, Pallas kernels for 0%

commit v1 on v0

--- a/solution.py
+++ b/solution.py
@@ -2,6 +2,13 @@
 import jax.numpy as jnp
 from jax import lax
 from jax.sharding import PartitionSpec as P
+
+
+def swap_blocks(block, name, split, join):
+    devices = lax.axis_size(name)
+    pieces = jnp.stack(jnp.split(block, devices, axis=split), axis=0)
+    pieces = lax.all_to_all(pieces, name, split_axis=0, concat_axis=0)
+    return jnp.concatenate(pieces, axis=join)
 
 
 def laid_out(tiles, dim):
@@ -115,7 +122,7 @@
     own_heads = head_count // seg_count
     received = (
         *side_by_side((peaks[None], totals[None]), "seg", 2, 0, 1),
-        lax.all_to_all(outputs[None], "seg", split_axis=2, concat_axis=0, tiled=True),
+        swap_blocks(outputs[None], "seg", 2, 0),
     )
     peak_all, total_all, out_all = received
     largest = jnp.max(peak_all, axis=0)

time: 188 us -> 180 us (0.957)
  other arithmetic: 27.5 us -> 6.05 us
  local copies, waits for them, and re-layouts: 31.1 us -> 46.8 us
  waiting for transfers between devices: 40.6 us -> 48 us
  matrix products: 15.5 us -> 10.9 us
  starting transfers between devices: 29.5 us -> 25 us
    unnamed x1 -> x0, other arithmetic: 19.4 us -> none
    unnamed x14 -> x44, local copies, waits for them, and re-layouts: 23 us -> 32 us
    all_to_all x1, waiting for transfers between devices: 0.01 us -> 7.7 us  [side_by_side(): lax.all_to_all(both, axis, split_axis=split_dim, concat_axis=concat_dim,...]
    dot_general x1, matrix products: 8.53 us -> 3.81 us  [one_doc(): jnp.einsum('qhk,khd->qhd', scaled, split_values, preferred_element_type=j...]
    all_to_all x1, starting transfers between devices: 8.15 us -> 3.93 us  [swap_blocks(): pieces = lax.all_to_all(pieces, name, split_axis=0, concat_axis=0)]
    mul x0 -> x2, local copies, waits for them, and re-layouts: none -> 3.59 us  [per_device(): out_all.reshape(seg_count, row_count, own_heads, head_dim)]
    all_to_all x1 -> x0, other arithmetic: 3.22 us -> none  [per_device(): lax.all_to_all(outputs[None], 'seg', split_axis=2, concat_axis=0, tiled=T...]
    transpose x0 -> x1, local copies, waits for them, and re-layouts: none -> 2.85 us  [one_doc(): jnp.einsum('qhk,khd->qhd', scaled, split_values, preferred_element_type=j...]
  transfers between devices with their start and end apart: 5 -> 5, of which waited for: 3 -> 4; matrix products, arithmetic and copies ran while one was open for 29% -> 11% of each run, Pallas kernels for 0% -> 0%
where the time goes in v1:
time: 180 us; the launch traced here: 179 us
  waiting for transfers between devices  48 us (27%)
  local copies, waits for them, and re-layouts  46.8 us (26%)
  blocking collectives  41.7 us (23%)
  starting transfers between devices  25 us (14%)
  matrix products  10.9 us (6%)
  other arithmetic  6.05 us (3%)
    unnamed x44, local copies, waits for them, and re-layouts  32 us
    all_to_all x3, waiting for transfers between devices, from_everyone(): lax.all_to_all(jnp.broadcast_to(shard[None], (count, *shard.shape)), axis...  25.6 us
    all_to_all x1, blocking collectives, sent_and_summed(): lax.all_to_all(tiles, axis, split_axis=0, concat_axis=0, tiled=True)  21.1 us
    all_to_all x1, blocking collectives, from_everyone(): lax.all_to_all(jnp.broadcast_to(shard[None], (count, *shard.shape)), axis...  20.6 us
    all_to_all x1, waiting for transfers between devices, swap_blocks(): pieces = lax.all_to_all(pieces, name, split_axis=0, concat_axis=0)  14.7 us
    all_to_all x3, starting transfers between devices, from_everyone(): lax.all_to_all(jnp.broadcast_to(shard[None], (count, *shard.shape)), axis...  12.8 us
    all_to_all x1, starting transfers between devices, side_by_side(): lax.all_to_all(both, axis, split_axis=split_dim, concat_axis=concat_dim,...  8.33 us
    all_to_all x1, waiting for transfers between devices, side_by_side(): lax.all_to_all(both, axis, split_axis=split_dim, concat_axis=concat_dim,...  7.7 us
  transfers between devices with their start and end apart: 5, of which 4 were waited for; matrix products, arithmetic and copies ran while one was open for 11% of the time, Pallas kernels for 0%

profile of v1, /device:TPU:0, one launch (start us, length us, event | category | flops | bytes accessed | tf_op | source)
XLA Modules:
  0.0 179.3 jit_solution(12158617641739664484)
XLA Ops:
  0.9 20.6 %all_to_all.48 = bf16[32,64,128]{2,1,0:T(8,128)(2,1)S(1)} all-to-all(bf16[32,64,128]{2,1,0:T(8,128)(2,1)S(1)} %broadcast_in_dim.84), channel_id=1, replica_groups=mesh['seg'=32,'rep'=4] {'seg'}, dimensions={0} | all-to-all | bytes 1048576 | tf_op jit(solution)/shard_map/all_to_all | solution.py:22
  21.5 2.1 %broadcast_in_dim.85 = bf16[4,1024,128]{2,1,0:T(8,128)(2,1)} broadcast(bf16[1024,128]{1,0:T(8,128)(2,1)} %param.11), dimensions={1,2} | broadcast | bytes 1310720 | tf_op jit(solution)/shard_map/broadcast_in_dim | solution.py:23
  23.5 4.2 %all-to-all-start.1 = ((bf16[4,1024,128]{2,1,0:T(8,128)(2,1)}), bf16[4,1024,128]{2,1,0:T(8,128)(2,1)S(1)}, u32[]{:S(2)}, u32[]{:S(2)}) async-start(bf16[4,1024,128]{2,1,0:T(8,128)(2,1)} %broadcast_in_dim.85), calls=%async_computation.1 | async-start | bytes 2097152 | tf_op jit(solution)/shard_map/all_to_all | solution.py:22
  27.9 15.7 %all-to-all-done.1 = bf16[4,1024,128]{2,1,0:T(8,128)(2,1)S(1)} async-done(((bf16[4,1024,128]{2,1,0:T(8,128)(2,1)}), bf16[4,1024,128]{2,1,0:T(8,128)(2,1)S(1)}, u32[]{:S(2)}, u32[]{:S(2)}) %all-to-all-start.1) | async-done | bytes 1048608 | tf_op jit(solution)/shard_map/all_to_all | solution.py:22
  43.6 1.1 convolution_convert_fusion
  45.7 4.2 %all-to-all-start.2 = ((bf16[32,64,128]{2,1,0:T(8,128)(2,1)}), bf16[32,64,128]{2,1,0:T(8,128)(2,1)S(1)}, u32[]{:S(2)}, u32[]{:S(2)}) async-start(bf16[32,64,128]{2,1,0:T(8,128)(2,1)} %broadcast_in_dim.86), calls=%async_computation.2 | async-start | bytes 1048576 | tf_op jit(solution)/shard_map/all_to_all | solution.py:22
  50.8 6.6 %copy.28 = bf16[1,512,4096]{1,2,0:T(8,128)(2,1)} copy(bf16[1,512,4096]{2,1,0:T(8,128)(2,1)} %param.12) | data formatting | bytes 8388608 | tf_op args[3]
  57.3 6.5 %copy.33 = bf16[1,512,4096]{1,2,0:T(8,128)(2,1)} copy(bf16[1,512,4096]{2,1,0:T(8,128)(2,1)} %param.14) | data formatting | bytes 8388608 | tf_op args[5]
  64.8 4.3 %bitcast_reduce_fusion = (f32[64,64]{0,1:T(8,128)S(1)}, f32[64,64,512]{2,1,0:T(8,128)S(1)}) fusion(f32[64,512]{1,0:T(8,128)S(1)} %get-tuple-element.30, pred[512]{0:T(512)(128)(4,1)S(1)} %add_compare_fusion, bf16[512,64,64]{0,2,1:T(8,128)(2,1)} %bitcast.196, bf16[64,64,64]{2,1,0:T(8,128)(2,1)S(1)} %reshape.89), kind=kOutput, calls=%fused_computation.1 | convolution fusion | flops 274722816 | bytes 13255168 | tf_op jit(solution)/shard_map/while/body/eval_jaxpr/qhd,khd->qhk/dot_general | solution.py:97
  69.2 2.8 %fusion.2 = f32[64,64]{0,1:T(8,128)S(1)} fusion(f32[64,64,512]{2,1,0:T(8,128)S(1)} %get-tuple-element.28, f32[64,64]{0,1:T(8,128)S(1)} %get-tuple-element.27, f32[64,512]{1,0:T(8,128)S(1)} %get-tuple-element.30, pred[512]{0:T(512)(128)(4,1)S(1)} %add_compare_fusion), kind=kLoop, calls=%fused_computation.6 | loop fusion | flops 10481664 | bytes 8552960 | tf_op jit(solution)/shard_map/while/body/eval_jaxpr/reduce_sum | solution.py:107
  72.0 3.8 %fusion.11 = f32[64,64,64]{2,0,1:T(8,128)} fusion(bf16[512,64,64]{0,2,1:T(8,128)(2,1)S(1)} %bitcast.197, f32[64,64,512]{2,1,0:T(8,128)S(1)} %get-tuple-element.28, f32[64,512]{1,0:T(8,128)S(1)} %get-tuple-element.29, f32[64,64]{0,1:T(8,128)S(1)} %get-tuple-element.27, f32[64,512]{1,0:T(8,128)S(1)} %get-tuple-element.30, pred[512]{0:T(512)(128)(4,1)S(1)} %add_compare_fusion), kind=kOutput, calls=%fused_computation.15 | convolution fusion | flops 281018368 | bytes 13910528 | tf_op jit(solution)/shard_map/while/body/eval_jaxpr/qhk,khd->qhd/dot_general | solution.py:109
  75.8 2.9 %copy.34 = f32[64,64,64]{2,1,0:T(8,128)S(1)} copy(f32[64,64,64]{2,0,1:T(8,128)} %fusion.11) | data formatting | bytes 2097152 | tf_op jit(solution)/shard_map/while/body/eval_jaxpr/qhk,khd->qhd/transpose | solution.py:109
  98.9 8.3 %all-to-all-start.4 = ((f32[1,128,64]{1,0,2:T(1,128)}), f32[1,128,64]{1,0,2:T(1,128)S(1)}, u32[]{:S(2)}, u32[]{:S(2)}) async-start(f32[1,128,64]{1,0,2:T(1,128)} %pad_maximum_fusion), calls=%async_computation.4 | async-start | bytes 65536 | tf_op jit(solution)/shard_map/all_to_all | solution.py:39
  107.8 7.7 %all-to-all-done.4 = f32[1,128,64]{1,0,2:T(1,128)S(1)} async-done(((f32[1,128,64]{1,0,2:T(1,128)}), f32[1,128,64]{1,0,2:T(1,128)S(1)}, u32[]{:S(2)}, u32[]{:S(2)}) %all-to-all-start.4) | async-done | bytes 32800 | tf_op jit(solution)/shard_map/all_to_all | solution.py:39
  115.5 3.9 %all-to-all-start.3 = ((f32[32,1,64,128]{3,2,1,0:T(8,128)}), f32[32,1,64,128]{3,2,1,0:T(8,128)S(1)}, u32[]{:S(2)}, u32[]{:S(2)}) async-start(f32[32,1,64,128]{3,2,1,0:T(8,128)} %constant_dynamic-update-slice_fusion), calls=%async_computation.3 | async-start | bytes 2097152 | tf_op jit(solution)/shard_map/all_to_all | solution.py:10
  119.6 14.7 %all-to-all-done.3 = f32[32,1,64,128]{3,2,1,0:T(8,128)S(1)} async-done(((f32[32,1,64,128]{3,2,1,0:T(8,128)}), f32[32,1,64,128]{3,2,1,0:T(8,128)S(1)}, u32[]{:S(2)}, u32[]{:S(2)}) %all-to-all-start.3) | async-done | bytes 1048608 | tf_op jit(solution)/shard_map/all_to_all | solution.py:10
  134.3 1.3 broadcast_in_dim.94
  135.6 4.4 %all-to-all-start.5 = ((bf16[4,128,1024]{1,2,0:T(8,128)(2,1)}), bf16[4,128,1024]{1,2,0:T(8,128)(2,1)}, u32[]{:S(2)}, u32[]{:S(2)}) async-start(bf16[4,128,1024]{1,2,0:T(8,128)(2,1)} %broadcast_in_dim.94), calls=%async_computation.5 | async-start | bytes 2097152 | tf_op jit(solution)/shard_map/all_to_all | solution.py:22
  140.6 2.5 %mul.80 = f32[32,64,2,64]{3,2,1,0:T(2,128)S(1)} broadcast(f32[32,64,2]{2,1,0:T(8,128)S(1)} %copy.35), dimensions={0,1,2} | broadcast | bytes 1064960 | tf_op jit(solution)/shard_map/mul | solution.py:132
  143.1 1.1 mul.81
  144.3 1.3 multiply_reduce_fusion
  146.0 9.9 %all-to-all-done.5 = bf16[4,128,1024]{1,2,0:T(8,128)(2,1)} async-done(((bf16[4,128,1024]{1,2,0:T(8,128)(2,1)}), bf16[4,128,1024]{1,2,0:T(8,128)(2,1)}, u32[]{:S(2)}, u32[]{:S(2)}) %all-to-all-start.5) | async-done | bytes 1048608 | tf_op jit(solution)/shard_map/all_to_all | solution.py:22
  155.8 1.7 convolution_bitcast_fusion
  157.5 21.1 %all_to_all.49 = f32[32,64,128]{2,1,0:T(8,128)S(1)} all-to-all(f32[32,64,128]{2,1,0:T(8,128)S(1)} %convolution_bitcast_fusion), channel_id=1, replica_groups=mesh['seg'=32,'rep'=4] {'seg'}, dimensions={0} | all-to-all | bytes 2097152 | tf_op jit(solution)/shard_map/all_to_all | solution.py:53
  (66 shorter events, 25.9 us)
Async XLA Ops:
  0.0 49.9 %copy-start.3 = (f32[1,4,64]{2,1,0:T(4,128)S(1)}, f32[1,4,64]{2,1,0:T(4,128)}, u32[]{:S(2)}) copy-start(f32[1,4,64]{2,1,0:T(4,128)} %param.13) | copy-start | bytes 3076
  0.0 50.0 %copy-start.4 = (f32[1,4,64]{2,1,0:T(4,128)S(1)}, f32[1,4,64]{2,1,0:T(4,128)}, u32[]{:S(2)}) copy-start(f32[1,4,64]{2,1,0:T(4,128)} %param.15) | copy-start | bytes 3076
  23.5 20.1 %all-to-all-start.1 = ((bf16[4,1024,128]{2,1,0:T(8,128)(2,1)}), bf16[4,1024,128]{2,1,0:T(8,128)(2,1)S(1)}, u32[]{:S(2)}, u32[]{:S(2)}) async-start(bf16[4,1024,128]{2,1,0:T(8,128)(2,1)} %broadcast_in_dim.85), calls=%async_computation.1 | async-start | bytes 2097152 | tf_op jit(solution)/shard_map/all_to_all | solution.py:22
  45.7 18.4 %all-to-all-start.2 = ((bf16[32,64,128]{2,1,0:T(8,128)(2,1)}), bf16[32,64,128]{2,1,0:T(8,128)(2,1)S(1)}, u32[]{:S(2)}, u32[]{:S(2)}) async-start(bf16[32,64,128]{2,1,0:T(8,128)(2,1)} %broadcast_in_dim.86), calls=%async_computation.2 | async-start | bytes 1048576 | tf_op jit(solution)/shard_map/all_to_all | solution.py:22
  64.8 7.1 %copy-start = (bf16[1,512,4096]{1,2,0:T(8,128)(2,1)S(1)}, bf16[1,512,4096]{1,2,0:T(8,128)(2,1)}, u32[]{:S(2)}) copy-start(bf16[1,512,4096]{1,2,0:T(8,128)(2,1)} %copy.33) | copy-start | bytes 12582916
  75.8 43.7 %copy-start.2 = (bf16[128,1024]{1,0:T(8,128)(2,1)S(1)}, bf16[128,1024]{1,0:T(8,128)(2,1)}, u32[]{:S(2)}) copy-start(bf16[128,1024]{1,0:T(8,128)(2,1)} %param.17) | copy-start | bytes 786436
  98.9 16.6 %all-to-all-start.4 = ((f32[1,128,64]{1,0,2:T(1,128)}), f32[1,128,64]{1,0,2:T(1,128)S(1)}, u32[]{:S(2)}, u32[]{:S(2)}) async-start(f32[1,128,64]{1,0,2:T(1,128)} %pad_maximum_fusion), calls=%async_computation.4 | async-start | bytes 65536 | tf_op jit(solution)/shard_map/all_to_all | solution.py:39
  115.5 18.8 %all-to-all-start.3 = ((f32[32,1,64,128]{3,2,1,0:T(8,128)}), f32[32,1,64,128]{3,2,1,0:T(8,128)S(1)}, u32[]{:S(2)}, u32[]{:S(2)}) async-start(f32[32,1,64,128]{3,2,1,0:T(8,128)} %constant_dynamic-update-slice_fusion), calls=%async_computation.3 | async-start | bytes 2097152 | tf_op jit(solution)/shard_map/all_to_all | solution.py:10
  134.3 5.8 %copy-start.1 = (f32[32,1,64,128]{3,2,1,0:T(8,128)}, f32[32,1,64,128]{3,2,1,0:T(8,128)S(1)}, u32[]{:S(2)}) copy-start(f32[32,1,64,128]{3,2,1,0:T(8,128)S(1)} %all-to-all-done.3) | copy-start | bytes 3145732
  135.6 20.2 %all-to-all-start.5 = ((bf16[4,128,1024]{1,2,0:T(8,128)(2,1)}), bf16[4,128,1024]{1,2,0:T(8,128)(2,1)}, u32[]{:S(2)}, u32[]{:S(2)}) async-start(bf16[4,128,1024]{1,2,0:T(8,128)(2,1)} %broadcast_in_dim.94), calls=%async_computation.5 | async-start | bytes 2097152 | tf_op jit(solution)/shard_map/all_to_all | solution.py:22
